TPU v7x, 32 devices: a whole 2x2x4 slice. The times are simulated.
32 devices in a mesh: row: 2 (over x), col: 16 (over z, y, core).
Axes of the slice: x: 2, y: 2, z: 4, core: 2. Of those that a mesh axis runs over, the one named last changes fastest.
Arguments:
- adjacency: int32 [2048, 64], P('row', 'col'), may hold values from -2147483648 to 2147483647, as said below
- tile_mask: int32 [16, 16], P('row', 'col'), may hold values from 0 to 1, as said below
- thresholds: int32 [3], replicated, may hold values from 30 to 61
Outputs:
- truss_support: float32 [2048, 2048], P('row', 'col')
- edge_counts: int32 [3], replicated
Inputs may be any that keep to these rules, and one draw needn't show every extreme that they name: The graph of adjacency is symmetric with an empty diagonal: bit b of word w of row i equals the bit for row 32 w + b and column i. `tile_mask`: Symmetric.
All inputs are finite; a program needn't handle non-finite values.
Results may differ from a plain program's by a relative error of at most 0.0003.
Values may be sent and summed in bfloat16 or wider, within the bound.
No kernel may reach another device: no remote copies, remote signals or barrier semaphores. Data moves between devices by JAX's collectives and lax.ppermute only.
A program may use at most 64 MiB of HBM per device.

v0:
```python
import jax
import jax.numpy as jnp
from jax import lax
from jax.sharding import PartitionSpec as P

TILE = 128
ITERS = 3


def unpack_bits(packed_rows):
    shifts = jnp.arange(32, dtype=jnp.int32)
    flat_bits = jnp.bitwise_and(jnp.right_shift(packed_rows[:, :, None], shifts), 1)
    return flat_bits.reshape(packed_rows.shape[0], packed_rows.shape[1] * 32)


def pack_bits(flat_bits):
    shifts = jnp.arange(32, dtype=jnp.int32)
    grouped = flat_bits.reshape(flat_bits.shape[0], flat_bits.shape[1] // 32, 32)
    return jnp.sum(jnp.left_shift(grouped, shifts), axis=-1, dtype=jnp.int32)


def block_product(packed_rows, matching):
    operand = unpack_bits(packed_rows).astype(jnp.bfloat16)
    return jnp.dot(operand, matching, preferred_element_type=jnp.float32)


def local(adjacency, tile_mask, thresholds):
    rows_here = adjacency.shape[0]
    cols_here = adjacency.shape[1] * 32
    flat_bits = unpack_bits(adjacency)
    tile_cover = jnp.broadcast_to(
        tile_mask[:, None, :, None], (tile_mask.shape[0], TILE, tile_mask.shape[1], TILE)
    )
    surviving = flat_bits * tile_cover.reshape(rows_here, cols_here)
    survived_list = []
    support = jnp.zeros((rows_here, cols_here), jnp.float32)
    for iteration in range(ITERS):
        packed_here = pack_bits(surviving)
        column_words = lax.all_gather(packed_here, "row", axis=0, tiled=True)
        column_bits = unpack_bits(column_words)
        lower_panel = column_bits.astype(jnp.bfloat16)
        wedge_counts = block_product(
            lax.all_gather(packed_here, "col", axis=1, tiled=True), lower_panel
        )
        support = wedge_counts * surviving.astype(jnp.float32)
        retained = (support >= thresholds[iteration].astype(jnp.float32)).astype(jnp.int32)
        surviving = surviving * retained
        survived = jnp.sum(surviving)
        survived_list.append(survived)
    edge_counts = lax.psum(jnp.stack(survived_list), ("row", "col"))
    truss_support = (
        support * surviving.astype(jnp.float32) / thresholds[ITERS - 1].astype(jnp.float32)
    )
    return (truss_support, edge_counts)


def solution(mesh):
    in_specs = (P("row", "col"), P("row", "col"), P())
    out_specs = (P("row", "col"), P())
    return jax.shard_map(local, mesh=mesh, in_specs=in_specs, out_specs=out_specs, check_vma=False)
```

profile of v0, /device:TPU:14, one launch (start us, length us, event | category | flops | bytes accessed | tf_op | source)
XLA Modules:
  0.0 131.3 jit_solution(8113006497730622411)
XLA Ops:
  0.6 0.6 copy-done
  1.3 1.3 %fusion.8 = (s32[1]{0:T(128)}, s32[1]{0:T(128)}, s32[1]{0:T(128)}) fusion(s32[3]{0:T(128)} %param.5), kind=kLoop, calls=%fused_computation.25 | loop fusion | bytes 24 | tf_op jit(solution)/shard_map/slice | solution.py:46
  4.7 0.8 shift-left_reduce_fusion.2
  5.5 4.4 %all_gather.19 = s32[2048,4]{0,1:T(4,128)S(1)} all-gather(s32[1024,4]{0,1:T(4,128)S(1)} %shift-left_reduce_fusion.2), channel_id=1, replica_groups=mesh['row'=2,'col'=16] {'row'}, dimensions={0}, use_global_device_ids=true | all-gather | bytes 49152 | tf_op jit(solution)/shard_map/all_gather | solution.py:39
  9.9 15.8 %all-gather = s32[16,4,1024]{2,1,0:T(4,128)S(1)} all-gather(s32[1,4,1024]{2,1,0:T(4,128)S(1)} %bitcast.55), channel_id=1, replica_groups=mesh['row'=2,'col'=16] {'col'}, dimensions={0}, use_global_device_ids=true | all-gather | bytes 278528 | tf_op jit(solution)/shard_map/all_gather | solution.py:43
  25.8 0.1 and_convert_fusion.5
  26.0 0.8 fusion.5
  26.8 1.6 %and_convert_fusion.2 = bf16[1024,64,32]{0,2,1:T(8,128)(2,1)S(1)} fusion(s32[1024,64]{0,1:T(8,128)S(1)} %bitcast.49), kind=kLoop, calls=%fused_computation.2 | loop fusion | flops 6291456 | bytes 4456448 | tf_op jit(solution)/shard_map/convert_element_type | solution.py:23
  28.4 0.9 shift-left_reduce_fusion.1
  29.3 0.8 reduce_sum.57
  30.0 4.4 %all_gather.21 = s32[2048,4]{0,1:T(4,128)S(1)} all-gather(s32[1024,4]{0,1:T(4,128)S(1)} %get-tuple-element.13), channel_id=1, replica_groups=mesh['row'=2,'col'=16] {'row'}, dimensions={0}, use_global_device_ids=true | all-gather | bytes 49152 | tf_op jit(solution)/shard_map/all_gather | solution.py:39
  34.4 22.1 %all-gather.1 = s32[16,4,1024]{2,1,0:T(4,128)S(1)} all-gather(s32[1,4,1024]{2,1,0:T(4,128)S(1)} %bitcast.53), channel_id=1, replica_groups=mesh['row'=2,'col'=16] {'col'}, dimensions={0}, use_global_device_ids=true | all-gather | bytes 278528 | tf_op jit(solution)/shard_map/all_gather | solution.py:43
  56.6 0.1 and_convert_fusion.4
  56.8 1.6 %and_convert_fusion.1 = bf16[1024,64,32]{0,2,1:T(8,128)(2,1)S(1)} fusion(s32[1024,64]{0,1:T(8,128)S(1)} %bitcast.50), kind=kLoop, calls=%fused_computation.1 | loop fusion | flops 6291456 | bytes 4456448 | tf_op jit(solution)/shard_map/convert_element_type | solution.py:23
  58.3 0.9 shift-left_reduce_fusion
  59.3 4.4 %all_gather.23 = s32[2048,4]{0,1:T(4,128)S(1)} all-gather(s32[1024,4]{0,1:T(4,128)S(1)} %get-tuple-element.15), channel_id=1, replica_groups=mesh['row'=2,'col'=16] {'row'}, dimensions={0}, use_global_device_ids=true | all-gather | bytes 49152 | tf_op jit(solution)/shard_map/all_gather | solution.py:39
  63.7 17.7 %all-gather.2 = s32[16,4,1024]{2,1,0:T(4,128)S(1)} all-gather(s32[1,4,1024]{2,1,0:T(4,128)S(1)} %bitcast.54), channel_id=1, replica_groups=mesh['row'=2,'col'=16] {'col'}, dimensions={0}, use_global_device_ids=true | all-gather | bytes 278528 | tf_op jit(solution)/shard_map/all_gather | solution.py:43
  81.5 0.1 and_convert_fusion.3
  81.6 1.6 %and_convert_fusion = bf16[1024,64,32]{0,2,1:T(8,128)(2,1)S(1)} fusion(s32[1024,64]{0,1:T(8,128)S(1)} %bitcast.51), kind=kLoop, calls=%fused_computation | loop fusion | flops 6291456 | bytes 4456448 | tf_op jit(solution)/shard_map/convert_element_type | solution.py:23
  83.2 0.9 multiply_divide_fusion
  84.0 0.9 fusion.7
  84.9 2.0 %pad_add_fusion = s32[3]{0:T(128)S(1)} fusion(s32[1]{0:T(128)} %bitcast.25, s32[1]{0:T(128)} %bitcast.24, s32[1]{0:T(128)} %bitcast.23), kind=kLoop, calls=%fused_computation.23 | loop fusion | flops 6 | bytes 24 | tf_op jit(solution)/shard_map/stack | solution.py:50
  86.9 1.0 copy.11
  87.9 43.4 %psum.7 = s32[3]{0:T(128)} all-reduce(s32[3]{0:T(128)S(1)} %pad_add_fusion), channel_id=1, replica_groups=mesh['row'=2,'col'=16] {'row','col'}, use_global_device_ids=true, to_apply=%region_6.0 | all-reduce | flops 3 | bytes 24 | tf_op jit(solution)/shard_map/psum | solution.py:50
  (7 shorter events, 0.4 us)
Async XLA Ops:
  0.6 0.7 copy-start
where the time goes:
time: 132 us; the launch traced here: 131 us
  blocking collectives  112 us (85%)
  other arithmetic  10.3 us (8%)
  local copies, waits for them, and re-layouts  3.42 us (3%)
  matrix products  2.66 us (2%)
  between operations  2.59 us (2%)
    all_gather x3, blocking collectives, local(): lax.all_gather(packed_here, 'col', axis=1, tiled=True)  55.6 us
    psum x1, blocking collectives, local(): edge_counts = lax.psum(jnp.stack(survived_list), ('row', 'col'))  43.4 us
    all_gather x3, blocking collectives, local(): column_words = lax.all_gather(packed_here, 'row', axis=0, tiled=True)  13.2 us
    convert_element_type x3, other arithmetic, block_product(): operand = unpack_bits(packed_rows).astype(jnp.bfloat16)  4.67 us
    dot_general x3, matrix products, block_product(): return jnp.dot(operand, matching, preferred_element_type=jnp.float32)  2.66 us

commit v1 on v0

--- a/solution.py
+++ b/solution.py
@@ -5,6 +5,18 @@
 
 TILE = 128
 ITERS = 3
+
+
+def doubled_up(shard, axis, dim):
+    ways, here, hop = (lax.axis_size(axis), lax.axis_index(axis), shard.shape[dim])
+    line, have = (shard, 1)
+    while have < ways:
+        line = jnp.concatenate(
+            [line, lax.ppermute(line, axis, [(d, (d - have) % ways) for d in range(ways)])],
+            axis=dim,
+        )
+        have = 2 * have
+    return jnp.roll(line, here * hop, axis=dim)
 
 
 def unpack_bits(packed_rows):
@@ -39,9 +51,7 @@
         column_words = lax.all_gather(packed_here, "row", axis=0, tiled=True)
         column_bits = unpack_bits(column_words)
         lower_panel = column_bits.astype(jnp.bfloat16)
-        wedge_counts = block_product(
-            lax.all_gather(packed_here, "col", axis=1, tiled=True), lower_panel
-        )
+        wedge_counts = block_product(doubled_up(packed_here, "col", 1), lower_panel)
         support = wedge_counts * surviving.astype(jnp.float32)
         retained = (support >= thresholds[iteration].astype(jnp.float32)).astype(jnp.int32)
         surviving = surviving * retained

time: 132 us -> 127 us (0.962)
  blocking collectives: 112 us -> 55 us
  starting transfers between devices: 0 us -> 26.1 us
  waiting for transfers between devices: 0 us -> 25.9 us
    all_gather x3 -> x0, blocking collectives: 55.6 us -> none  [local(): lax.all_gather(packed_here, 'col', axis=1, tiled=True)]
    ppermute x0 -> x12, starting transfers between devices: none -> 26.1 us  [doubled_up(): lax.ppermute(line, axis, [(d, (d - have) % ways) for d in range(ways)])]
    ppermute x0 -> x12, waiting for transfers between devices: none -> 25.9 us  [doubled_up(): lax.ppermute(line, axis, [(d, (d - have) % ways) for d in range(ways)])]
    psum x1, blocking collectives: 43.4 us -> 41.8 us  [local(): edge_counts = lax.psum(jnp.stack(survived_list), ('row', 'col'))]
  transfers between devices with their start and end apart: 0 -> 12, of which waited for: 0 -> 9; matrix products, arithmetic and copies ran while one was open for 0% -> 3% of each run, Pallas kernels for 0% -> 0%
where the time goes in v1:
time: 127 us
  blocking collectives  55 us (43%)
  starting transfers between devices  26.1 us (21%)
  waiting for transfers between devices  25.9 us (20%)
  other arithmetic  10.7 us (8%)
  local copies, waits for them, and re-layouts  3.35 us (3%)
  between operations  2.84 us (2%)
  matrix products  2.72 us (2%)
    psum x1, blocking collectives, local(): edge_counts = lax.psum(jnp.stack(survived_list), ('row', 'col'))  41.8 us
    ppermute x12, starting transfers between devices, doubled_up(): lax.ppermute(line, axis, [(d, (d - have) % ways) for d in range(ways)])  26.1 us
    ppermute x12, waiting for transfers between devices, doubled_up(): lax.ppermute(line, axis, [(d, (d - have) % ways) for d in range(ways)])  25.9 us
    all_gather x3, blocking collectives, local(): column_words = lax.all_gather(packed_here, 'row', axis=0, tiled=True)  13.2 us
    convert_element_type x3, other arithmetic, block_product(): operand = unpack_bits(packed_rows).astype(jnp.bfloat16)  4.67 us
    dot_general x3, matrix products, block_product(): return jnp.dot(operand, matching, preferred_element_type=jnp.float32)  2.72 us
  transfers between devices with their start and end apart: 12, of which 9 were waited for; matrix products, arithmetic and copies ran while one was open for 3% of the time, Pallas kernels for 0%

profile of v1, /device:TPU:14, one launch (start us, length us, event | category | flops | bytes accessed | tf_op | source)
XLA Modules:
  0.0 126.6 jit_solution(2455557141201165117)
XLA Ops:
  2.3 1.4 %collective-permute-done = s32[1024,4]{0,1:T(4,128)S(1)} collective-permute-done((s32[1024,4]{0,1:T(4,128)S(1)}, s32[1024,4]{0,1:T(4,128)S(1)}, u32[]{:S(2)}, u32[]{:S(2)}) %collective-permute-start) | collective-permute-done | bytes 16416 | tf_op jit(solution)/shard_map/ppermute | solution.py:15
  5.1 3.5 %collective-permute-done.1 = s32[1024,8]{0,1:T(8,128)S(1)} collective-permute-done((s32[1024,8]{0,1:T(8,128)S(1)}, s32[1024,8]{0,1:T(8,128)S(1)}, u32[]{:S(2)}, u32[]{:S(2)}) %collective-permute-start.1) | collective-permute-done | bytes 32800 | tf_op jit(solution)/shard_map/ppermute | solution.py:15
  8.6 1.8 %collective-permute-start.2 = (s32[1024,16]{0,1:T(8,128)S(1)}, s32[1024,16]{0,1:T(8,128)S(1)}, u32[]{:S(2)}, u32[]{:S(2)}) collective-permute-start(s32[1024,16]{0,1:T(8,128)S(1)} %pad_add_fusion.3), channel_id=1, source_target_pairs={{0,12},{1,13},{2,14},{3,15},{4,0},{5,1},{6,2},{7,3},{8,4},{9,5},{1... | collective-permute-start | bytes 196616 | tf_op jit(solution)/shard_map/ppermute | solution.py:15
  10.4 4.4 %all_gather.9 = s32[2048,4]{0,1:T(4,128)S(1)} all-gather(s32[1024,4]{0,1:T(4,128)S(1)} %shift-left_reduce_fusion.2), channel_id=1, replica_groups=mesh['row'=2,'col'=16] {'row'}, dimensions={0}, use_global_device_ids=true | all-gather | bytes 49152 | tf_op jit(solution)/shard_map/all_gather | solution.py:51
  14.8 4.4 %collective-permute-start.3 = (s32[1024,32]{0,1:T(8,128)S(1)}, s32[1024,32]{0,1:T(8,128)S(1)}, u32[]{:S(2)}, u32[]{:S(2)}) collective-permute-start(s32[1024,32]{0,1:T(8,128)S(1)} %pad_add_fusion), channel_id=1, source_target_pairs={{0,8},{1,9},{2,10},{3,11},{4,12},{5,13},{6,14},{7,15},{8,0},{9,1},... | collective-permute-start | bytes 393224 | tf_op jit(solution)/shard_map/ppermute | solution.py:15
  22.4 2.7 %collective-permute-done.3 = s32[1024,32]{0,1:T(8,128)S(1)} collective-permute-done((s32[1024,32]{0,1:T(8,128)S(1)}, s32[1024,32]{0,1:T(8,128)S(1)}, u32[]{:S(2)}, u32[]{:S(2)}) %collective-permute-start.3) | collective-permute-done | bytes 131104 | tf_op jit(solution)/shard_map/ppermute | solution.py:15
  25.2 1.6 %and_convert_fusion.2 = bf16[1024,64,32]{0,2,1:T(8,128)(2,1)S(1)} fusion(s32[1024,64]{0,1:T(8,128)S(1)} %fusion.9), kind=kLoop, calls=%fused_computation.2 | loop fusion | flops 6291456 | bytes 4456448 | tf_op jit(solution)/shard_map/convert_element_type | solution.py:35
  27.7 1.4 %collective-permute-done.4 = s32[1024,4]{0,1:T(4,128)S(1)} collective-permute-done((s32[1024,4]{0,1:T(4,128)S(1)}, s32[1024,4]{0,1:T(4,128)S(1)}, u32[]{:S(2)}, u32[]{:S(2)}) %collective-permute-start.4) | collective-permute-done | bytes 16416 | tf_op jit(solution)/shard_map/ppermute | solution.py:15
  29.2 3.9 %collective-permute-start.5 = (s32[1024,8]{0,1:T(8,128)S(1)}, s32[1024,8]{0,1:T(8,128)S(1)}, u32[]{:S(2)}, u32[]{:S(2)}) collective-permute-start(s32[1024,8]{0,1:T(8,128)S(1)} %pad_add_fusion.7), channel_id=1, source_target_pairs={{0,14},{1,15},{2,0},{3,1},{4,2},{5,3},{6,4},{7,5},{8,6},{9,7},{10,... | collective-permute-start | bytes 98312 | tf_op jit(solution)/shard_map/ppermute | solution.py:15
  33.1 1.6 %collective-permute-done.5 = s32[1024,8]{0,1:T(8,128)S(1)} collective-permute-done((s32[1024,8]{0,1:T(8,128)S(1)}, s32[1024,8]{0,1:T(8,128)S(1)}, u32[]{:S(2)}, u32[]{:S(2)}) %collective-permute-start.5) | collective-permute-done | bytes 32800 | tf_op jit(solution)/shard_map/ppermute | solution.py:15
  34.7 2.2 %collective-permute-start.6 = (s32[1024,16]{0,1:T(8,128)S(1)}, s32[1024,16]{0,1:T(8,128)S(1)}, u32[]{:S(2)}, u32[]{:S(2)}) collective-permute-start(s32[1024,16]{0,1:T(8,128)S(1)} %pad_add_fusion.4), channel_id=1, source_target_pairs={{0,12},{1,13},{2,14},{3,15},{4,0},{5,1},{6,2},{7,3},{8,4},{9,5},{1... | collective-permute-start | bytes 196616 | tf_op jit(solution)/shard_map/ppermute | solution.py:15
  37.6 4.4 %all_gather.10 = s32[2048,4]{0,1:T(4,128)S(1)} all-gather(s32[1024,4]{0,1:T(4,128)S(1)} %get-tuple-element.12), channel_id=1, replica_groups=mesh['row'=2,'col'=16] {'row'}, dimensions={0}, use_global_device_ids=true | all-gather | bytes 49152 | tf_op jit(solution)/shard_map/all_gather | solution.py:51
  42.0 3.4 %collective-permute-start.7 = (s32[1024,32]{0,1:T(8,128)S(1)}, s32[1024,32]{0,1:T(8,128)S(1)}, u32[]{:S(2)}, u32[]{:S(2)}) collective-permute-start(s32[1024,32]{0,1:T(8,128)S(1)} %pad_add_fusion.1), channel_id=1, source_target_pairs={{0,8},{1,9},{2,10},{3,11},{4,12},{5,13},{6,14},{7,15},{8,0},{9,1},... | collective-permute-start | bytes 393224 | tf_op jit(solution)/shard_map/ppermute | solution.py:15
  45.6 6.4 %collective-permute-done.7 = s32[1024,32]{0,1:T(8,128)S(1)} collective-permute-done((s32[1024,32]{0,1:T(8,128)S(1)}, s32[1024,32]{0,1:T(8,128)S(1)}, u32[]{:S(2)}, u32[]{:S(2)}) %collective-permute-start.7) | collective-permute-done | bytes 131104 | tf_op jit(solution)/shard_map/ppermute | solution.py:15
  52.1 1.6 %and_convert_fusion.1 = bf16[1024,64,32]{0,2,1:T(8,128)(2,1)S(1)} fusion(s32[1024,64]{0,1:T(8,128)S(1)} %fusion.8), kind=kLoop, calls=%fused_computation.1 | loop fusion | flops 6291456 | bytes 4456448 | tf_op jit(solution)/shard_map/convert_element_type | solution.py:35
  56.1 3.5 %collective-permute-start.9 = (s32[1024,8]{0,1:T(8,128)S(1)}, s32[1024,8]{0,1:T(8,128)S(1)}, u32[]{:S(2)}, u32[]{:S(2)}) collective-permute-start(s32[1024,8]{0,1:T(8,128)S(1)} %pad_add_fusion.8), channel_id=1, source_target_pairs={{0,14},{1,15},{2,0},{3,1},{4,2},{5,3},{6,4},{7,5},{8,6},{9,7},{10,... | collective-permute-start | bytes 98312 | tf_op jit(solution)/shard_map/ppermute | solution.py:15
  59.7 1.6 %collective-permute-done.9 = s32[1024,8]{0,1:T(8,128)S(1)} collective-permute-done((s32[1024,8]{0,1:T(8,128)S(1)}, s32[1024,8]{0,1:T(8,128)S(1)}, u32[]{:S(2)}, u32[]{:S(2)}) %collective-permute-start.9) | collective-permute-done | bytes 32800 | tf_op jit(solution)/shard_map/ppermute | solution.py:15
  61.3 2.6 %collective-permute-start.10 = (s32[1024,16]{0,1:T(8,128)S(1)}, s32[1024,16]{0,1:T(8,128)S(1)}, u32[]{:S(2)}, u32[]{:S(2)}) collective-permute-start(s32[1024,16]{0,1:T(8,128)S(1)} %pad_add_fusion.5), channel_id=1, source_target_pairs={{0,12},{1,13},{2,14},{3,15},{4,0},{5,1},{6,2},{7,3},{8,4},{9,5},{1... | collective-permute-start | bytes 196616 | tf_op jit(solution)/shard_map/ppermute | solution.py:15
  65.3 4.4 %all_gather.11 = s32[2048,4]{0,1:T(4,128)S(1)} all-gather(s32[1024,4]{0,1:T(4,128)S(1)} %get-tuple-element.14), channel_id=1, replica_groups=mesh['row'=2,'col'=16] {'row'}, dimensions={0}, use_global_device_ids=true | all-gather | bytes 49152 | tf_op jit(solution)/shard_map/all_gather | solution.py:51
  69.7 2.7 %collective-permute-start.11 = (s32[1024,32]{0,1:T(8,128)S(1)}, s32[1024,32]{0,1:T(8,128)S(1)}, u32[]{:S(2)}, u32[]{:S(2)}) collective-permute-start(s32[1024,32]{0,1:T(8,128)S(1)} %pad_add_fusion.2), channel_id=1, source_target_pairs={{0,8},{1,9},{2,10},{3,11},{4,12},{5,13},{6,14},{7,15},{8,0},{9,1},... | collective-permute-start | bytes 393224 | tf_op jit(solution)/shard_map/ppermute | solution.py:15
  72.5 5.8 %collective-permute-done.11 = s32[1024,32]{0,1:T(8,128)S(1)} collective-permute-done((s32[1024,32]{0,1:T(8,128)S(1)}, s32[1024,32]{0,1:T(8,128)S(1)}, u32[]{:S(2)}, u32[]{:S(2)}) %collective-permute-start.11) | collective-permute-done | bytes 131104 | tf_op jit(solution)/shard_map/ppermute | solution.py:15
  78.5 1.6 %and_convert_fusion = bf16[1024,64,32]{0,2,1:T(8,128)(2,1)S(1)} fusion(s32[1024,64]{0,1:T(8,128)S(1)} %fusion.7), kind=kLoop, calls=%fused_computation | loop fusion | flops 6291456 | bytes 4456448 | tf_op jit(solution)/shard_map/convert_element_type | solution.py:35
  81.8 2.0 %pad_add_fusion.9 = s32[3]{0:T(128)S(1)} fusion(s32[1]{0:T(128)} %bitcast.16, s32[1]{0:T(128)} %bitcast.15, s32[1]{0:T(128)} %bitcast.14), kind=kLoop, calls=%fused_computation.41 | loop fusion | flops 6 | bytes 24 | tf_op jit(solution)/shard_map/stack | solution.py:60
  84.8 41.8 %psum.7 = s32[3]{0:T(128)} all-reduce(s32[3]{0:T(128)S(1)} %pad_add_fusion.9), channel_id=1, replica_groups=mesh['row'=2,'col'=16] {'row','col'}, use_global_device_ids=true, to_apply=%region_6.8 | all-reduce | flops 3 | bytes 24 | tf_op jit(solution)/shard_map/psum | solution.py:60
  (40 shorter events, 13.1 us)
Async XLA Ops:
  0.6 0.7 copy-start
  2.2 1.5 %collective-permute-start = (s32[1024,4]{0,1:T(4,128)S(1)}, s32[1024,4]{0,1:T(4,128)S(1)}, u32[]{:S(2)}, u32[]{:S(2)}) collective-permute-start(s32[1024,4]{0,1:T(4,128)S(1)} %shift-left_reduce_fusion.2), channel_id=1, source_target_pairs={{0,15},{1,0},{2,1},{3,2},{4,3},{5,4},{6,5},{7,6},{8,7},{9,8},{10,9... | collective-permute-start | bytes 49160 | tf_op jit(solution)/shard_map/ppermute | solution.py:15
  3.7 4.9 %collective-permute-start.1 = (s32[1024,8]{0,1:T(8,128)S(1)}, s32[1024,8]{0,1:T(8,128)S(1)}, u32[]{:S(2)}, u32[]{:S(2)}) collective-permute-start(s32[1024,8]{0,1:T(8,128)S(1)} %pad_add_fusion.6), channel_id=1, source_target_pairs={{0,14},{1,15},{2,0},{3,1},{4,2},{5,3},{6,4},{7,5},{8,6},{9,7},{10,... | collective-permute-start | bytes 98312 | tf_op jit(solution)/shard_map/ppermute | solution.py:15
  8.6 6.2 %collective-permute-start.2 = (s32[1024,16]{0,1:T(8,128)S(1)}, s32[1024,16]{0,1:T(8,128)S(1)}, u32[]{:S(2)}, u32[]{:S(2)}) collective-permute-start(s32[1024,16]{0,1:T(8,128)S(1)} %pad_add_fusion.3), channel_id=1, source_target_pairs={{0,12},{1,13},{2,14},{3,15},{4,0},{5,1},{6,2},{7,3},{8,4},{9,5},{1... | collective-permute-start | bytes 196616 | tf_op jit(solution)/shard_map/ppermute | solution.py:15
  14.8 10.2 %collective-permute-start.3 = (s32[1024,32]{0,1:T(8,128)S(1)}, s32[1024,32]{0,1:T(8,128)S(1)}, u32[]{:S(2)}, u32[]{:S(2)}) collective-permute-start(s32[1024,32]{0,1:T(8,128)S(1)} %pad_add_fusion), channel_id=1, source_target_pairs={{0,8},{1,9},{2,10},{3,11},{4,12},{5,13},{6,14},{7,15},{8,0},{9,1},... | collective-permute-start | bytes 393224 | tf_op jit(solution)/shard_map/ppermute | solution.py:15
  27.7 1.5 %collective-permute-start.4 = (s32[1024,4]{0,1:T(4,128)S(1)}, s32[1024,4]{0,1:T(4,128)S(1)}, u32[]{:S(2)}, u32[]{:S(2)}) collective-permute-start(s32[1024,4]{0,1:T(4,128)S(1)} %get-tuple-element.12), channel_id=1, source_target_pairs={{0,15},{1,0},{2,1},{3,2},{4,3},{5,4},{6,5},{7,6},{8,7},{9,8},{10,9... | collective-permute-start | bytes 49160 | tf_op jit(solution)/shard_map/ppermute | solution.py:15
  29.2 5.5 %collective-permute-start.5 = (s32[1024,8]{0,1:T(8,128)S(1)}, s32[1024,8]{0,1:T(8,128)S(1)}, u32[]{:S(2)}, u32[]{:S(2)}) collective-permute-start(s32[1024,8]{0,1:T(8,128)S(1)} %pad_add_fusion.7), channel_id=1, source_target_pairs={{0,14},{1,15},{2,0},{3,1},{4,2},{5,3},{6,4},{7,5},{8,6},{9,7},{10,... | collective-permute-start | bytes 98312 | tf_op jit(solution)/shard_map/ppermute | solution.py:15
  34.7 7.3 %collective-permute-start.6 = (s32[1024,16]{0,1:T(8,128)S(1)}, s32[1024,16]{0,1:T(8,128)S(1)}, u32[]{:S(2)}, u32[]{:S(2)}) collective-permute-start(s32[1024,16]{0,1:T(8,128)S(1)} %pad_add_fusion.4), channel_id=1, source_target_pairs={{0,12},{1,13},{2,14},{3,15},{4,0},{5,1},{6,2},{7,3},{8,4},{9,5},{1... | collective-permute-start | bytes 196616 | tf_op jit(solution)/shard_map/ppermute | solution.py:15
  42.0 9.9 %collective-permute-start.7 = (s32[1024,32]{0,1:T(8,128)S(1)}, s32[1024,32]{0,1:T(8,128)S(1)}, u32[]{:S(2)}, u32[]{:S(2)}) collective-permute-start(s32[1024,32]{0,1:T(8,128)S(1)} %pad_add_fusion.1), channel_id=1, source_target_pairs={{0,8},{1,9},{2,10},{3,11},{4,12},{5,13},{6,14},{7,15},{8,0},{9,1},... | collective-permute-start | bytes 393224 | tf_op jit(solution)/shard_map/ppermute | solution.py:15
  54.6 1.5 %collective-permute-start.8 = (s32[1024,4]{0,1:T(4,128)S(1)}, s32[1024,4]{0,1:T(4,128)S(1)}, u32[]{:S(2)}, u32[]{:S(2)}) collective-permute-start(s32[1024,4]{0,1:T(4,128)S(1)} %get-tuple-element.14), channel_id=1, source_target_pairs={{0,15},{1,0},{2,1},{3,2},{4,3},{5,4},{6,5},{7,6},{8,7},{9,8},{10,9... | collective-permute-start | bytes 49160 | tf_op jit(solution)/shard_map/ppermute | solution.py:15
  56.1 5.1 %collective-permute-start.9 = (s32[1024,8]{0,1:T(8,128)S(1)}, s32[1024,8]{0,1:T(8,128)S(1)}, u32[]{:S(2)}, u32[]{:S(2)}) collective-permute-start(s32[1024,8]{0,1:T(8,128)S(1)} %pad_add_fusion.8), channel_id=1, source_target_pairs={{0,14},{1,15},{2,0},{3,1},{4,2},{5,3},{6,4},{7,5},{8,6},{9,7},{10,... | collective-permute-start | bytes 98312 | tf_op jit(solution)/shard_map/ppermute | solution.py:15
  61.3 8.4 %collective-permute-start.10 = (s32[1024,16]{0,1:T(8,128)S(1)}, s32[1024,16]{0,1:T(8,128)S(1)}, u32[]{:S(2)}, u32[]{:S(2)}) collective-permute-start(s32[1024,16]{0,1:T(8,128)S(1)} %pad_add_fusion.5), channel_id=1, source_target_pairs={{0,12},{1,13},{2,14},{3,15},{4,0},{5,1},{6,2},{7,3},{8,4},{9,5},{1... | collective-permute-start | bytes 196616 | tf_op jit(solution)/shard_map/ppermute | solution.py:15
  69.7 8.6 %collective-permute-start.11 = (s32[1024,32]{0,1:T(8,128)S(1)}, s32[1024,32]{0,1:T(8,128)S(1)}, u32[]{:S(2)}, u32[]{:S(2)}) collective-permute-start(s32[1024,32]{0,1:T(8,128)S(1)} %pad_add_fusion.2), channel_id=1, source_target_pairs={{0,8},{1,9},{2,10},{3,11},{4,12},{5,13},{6,14},{7,15},{8,0},{9,1},... | collective-permute-start | bytes 393224 | tf_op jit(solution)/shard_map/ppermute | solution.py:15
